TPU v7x, 32 devices: a whole 2x2x4 slice. The times are simulated.
32 devices in a mesh: dom: 8 (over z, x), sub: 4 (over y, core).
Axes of the slice: x: 2, y: 2, z: 4, core: 2. Of those that a mesh axis runs over, the one named last changes fastest.
Arguments:
- level_set: float32 [64, 32, 128], P('dom', 'sub'), may hold values from 0 to 1
- velocity: float32 [3, 64, 32, 128], P(None, 'dom', 'sub'), may hold values from -6 to 6
- source: float32 [64, 32, 128], P('dom', 'sub'), may hold values from -12 to 12
Outputs:
- new_level: float32 [64, 32, 128], P('dom', 'sub')
- pressure: float32 [64, 32, 128], P('dom', 'sub')
- correction: float32 [64, 32, 128], P('dom', 'sub')
All inputs are finite; a program needn't handle non-finite values.
Results may differ from a plain program's by a relative error of at most 0.0003.
Values sent between devices are 32-bit elements; how exact they have to be, the bound alone decides.
A program may use at most 64 MiB of HBM per device.

v0:
```python
import math
import jax
import jax.numpy as jnp
import numpy as np
from jax import lax
from jax.sharding import PartitionSpec as P

SWEEPS = 2
PITERS = 2
gll_nodes = [
    -1.0,
    -0.8717401485096066,
    -0.5917001814331423,
    -0.2092992179024789,
    0.2092992179024789,
    0.5917001814331423,
    0.8717401485096066,
    1.0,
]
advect_step = 0.05
reinit_step = 0.02
interface_width = 0.1
density_ratio = 9.0


def padded(x, sides, width):
    for axis, dim in sides:
        devices, length = (lax.axis_size(axis), x.shape[dim])
        up = [(i, (i + 1) % devices) for i in range(devices)]
        down = [(j, i) for i, j in up]
        last = lax.slice_in_dim(x, length - width, length, axis=dim)
        leading = lax.slice_in_dim(x, 0, width, axis=dim)
        before = lax.ppermute(last, axis, up)
        after = lax.ppermute(leading, axis, down)
        x = jnp.concatenate([before, x, after], axis=dim)
    return x


def tables():
    node_points = np.array(gll_nodes)
    poly_order = 7
    values_prev = np.ones(8)
    values_now = node_points.copy()
    for degree in range(1, poly_order):
        values_next = ((2 * degree + 1) * node_points * values_now - degree * values_prev) / (
            degree + 1
        )
        values_prev, values_now = (values_now, values_next)
    matrix = np.zeros((8, 8))
    for line in range(8):
        for column in range(8):
            if line != column:
                matrix[line, column] = values_now[line] / (
                    values_now[column] * (node_points[line] - node_points[column])
                )
    matrix[0, 0] = -poly_order * (poly_order + 1) / 4.0
    matrix[7, 7] = poly_order * (poly_order + 1) / 4.0
    weights = 2.0 / (poly_order * (poly_order + 1) * values_now**2)
    return (matrix, weights)


def point_tables(full_shape, weights):
    corner_count = np.array([2.0, 1.0, 1.0, 1.0, 1.0, 1.0, 1.0, 2.0])
    weight_lines = []
    count_lines = []
    for dim_index in (1, 2, 3):
        repeats = full_shape[dim_index] // 8
        weight_lines.append(jnp.asarray(np.tile(weights, repeats), jnp.float32))
        count_lines.append(jnp.asarray(np.tile(1.0 / corner_count, repeats), jnp.float32))
    weight_cube = (
        weight_lines[0][:, None, None]
        * weight_lines[1][None, :, None]
        * weight_lines[2][None, None, :]
    )[None]
    inv_mult = (
        count_lines[0][:, None, None]
        * count_lines[1][None, :, None]
        * count_lines[2][None, None, :]
    )[None]
    return (weight_cube, inv_mult)


def derive(values, dim_index, matrix):
    full_shape = values.shape
    highest = lax.Precision.HIGHEST
    if dim_index == 1:
        blocks = values.reshape((full_shape[0], full_shape[1] // 8, 8) + full_shape[2:])
        result = jnp.einsum(
            "baipq,ji->bajpq", blocks, jnp.asarray(matrix, jnp.float32), precision=highest
        )
    elif dim_index == 2:
        blocks = values.reshape(full_shape[:2] + (full_shape[2] // 8, 8, full_shape[3]))
        result = jnp.einsum(
            "bpaiq,ji->bpajq", blocks, jnp.asarray(matrix, jnp.float32), precision=highest
        )
    else:
        block_width = math.gcd(full_shape[3], 128)
        block_matrix = jnp.asarray(np.kron(np.eye(block_width // 8), matrix), jnp.float32)
        blocks = values.reshape(full_shape[:3] + (full_shape[3] // block_width, block_width))
        result = jnp.einsum("bpqai,ji->bpqaj", blocks, block_matrix, precision=highest)
    return result.reshape(full_shape)


def gradient(values, matrix):
    return [derive(values, 1, matrix), derive(values, 2, matrix), derive(values, 3, matrix)]


def join_edges(values, upper, lower, dim_index):
    position = lax.broadcasted_iota(jnp.int32, values.shape, dim_index) % 8
    return values + jnp.where(position == 7, upper, 0.0) + jnp.where(position == 0, lower, 0.0)


def fold_faces(widened, dim_index, length):
    values = lax.slice_in_dim(widened, 1, length + 1, axis=dim_index)
    upper = lax.slice_in_dim(widened, 2, length + 2, axis=dim_index)
    lower = lax.slice_in_dim(widened, 0, length, axis=dim_index)
    return join_edges(values, upper, lower, dim_index)


def fold_local(values, dim_index):
    upper = jnp.roll(values, -1, axis=dim_index)
    lower = jnp.roll(values, 1, axis=dim_index)
    return join_edges(values, upper, lower, dim_index)


def assemble(values):
    widened = padded(values, (("dom", 1),), 1)
    values = fold_faces(widened, 1, values.shape[1])
    widened = padded(values, (("sub", 2),), 1)
    values = fold_faces(widened, 2, values.shape[2])
    return fold_local(values, 3)


def both_sums(residual, precond, applied, inv_mult):
    return lax.psum(
        (jnp.sum(residual * precond * inv_mult), jnp.sum(precond * applied * inv_mult)),
        ("dom", "sub"),
    )


def local(level_set, velocity, source):
    matrix, weights = tables()
    phase_field = level_set[None]
    weight_cube, inv_mult = point_tables(phase_field.shape, weights)
    gradients = gradient(phase_field, matrix)
    advected = phase_field - advect_step * (
        velocity[0:1] * gradients[0] + velocity[1:2] * gradients[1] + velocity[2:3] * gradients[2]
    )
    phase_field = assemble(advected) * inv_mult
    gradients = gradient(phase_field, matrix)
    magnitude = jnp.sqrt(
        gradients[0] * gradients[0] + gradients[1] * gradients[1] + gradients[2] * gradients[2]
    )
    scaled = 1.0 / jnp.maximum(magnitude, 1.0)
    normals = [gradients[0] * scaled, gradients[1] * scaled, gradients[2] * scaled]
    for sweep_index in range(SWEEPS):
        if sweep_index > 0:
            gradients = gradient(phase_field, matrix)
        compress = phase_field * (1.0 - phase_field)
        change = derive(interface_width * gradients[0] - compress * normals[0], 1, matrix)
        change = change + derive(interface_width * gradients[1] - compress * normals[1], 2, matrix)
        change = change + derive(interface_width * gradients[2] - compress * normals[2], 3, matrix)
        phase_field = phase_field + reinit_step * assemble(change) * inv_mult
    mobility = 1.0 / (1.0 + density_ratio * phase_field * phase_field)
    weighted = weight_cube * mobility
    square_t = (matrix * matrix).T
    diag_local = (
        weight_cube
        + derive(weighted, 1, square_t)
        + derive(weighted, 2, square_t)
        + derive(weighted, 3, square_t)
    )
    assembled = assemble(jnp.concatenate([weight_cube * source[None], diag_local], axis=0))
    right_side = assembled[0:1]
    diagonal = assembled[1:2]
    transposed = matrix.T

    def operate(direction):
        grads_dir = gradient(direction, matrix)
        local_sum = weight_cube * direction + derive(weighted * grads_dir[0], 1, transposed)
        local_sum = (
            local_sum
            + derive(weighted * grads_dir[1], 2, transposed)
            + derive(weighted * grads_dir[2], 3, transposed)
        )
        return assemble(local_sum)

    solution = jnp.zeros_like(right_side)
    residual = right_side
    precond = residual / diagonal
    applied = operate(precond)
    norm_now, product = both_sums(residual, precond, applied, inv_mult)
    step_size = norm_now / product
    direction = precond
    along_image = applied
    for step_index in range(PITERS):
        solution = solution + step_size * direction
        residual = residual - step_size * along_image
        if step_index + 1 < PITERS:
            precond = residual / diagonal
            applied = operate(precond)
            norm_next, product = both_sums(residual, precond, applied, inv_mult)
            ratio_new = norm_next / norm_now
            step_size = norm_next / (product - ratio_new * norm_next / step_size)
            direction = precond + ratio_new * direction
            along_image = applied + ratio_new * along_image
            norm_now = norm_next
    return (phase_field[0], solution[0], (residual / diagonal)[0])


def solution(mesh):
    return jax.shard_map(
        local,
        mesh=mesh,
        in_specs=(P("dom", "sub", None), P(None, "dom", "sub", None), P("dom", "sub", None)),
        out_specs=(P("dom", "sub", None), P("dom", "sub", None), P("dom", "sub", None)),
        check_vma=False,
    )
```

profile of v0, /device:TPU:14, one launch (start us, length us, event | category | flops | bytes accessed | tf_op | source)
XLA Modules:
  0.0 165.5 jit_solution(13758522378719981348)
XLA Ops:
  0.7 0.8 fusion.168
  1.8 0.7 copy-done
  2.8 0.6 collective-permute-start
  3.3 2.4 %collective-permute-start.1 = (f32[1,1,8,128]{3,1,2,0:T(1,128)S(1)}, f32[1,1,8,128]{3,1,2,0:T(1,128)S(1)}, u32[]{:S(2)}, u32[]{:S(2)}) collective-permute-start(f32[1,1,8,128]{3,1,2,0:T(1,128)S(1)} %get-tuple-element.74), channel_id=1, source_target_pairs={{0,4},{4,8},{8,12},{12,16},{16,20},{20,24},{24,28},{28,0},{1,5},{5... | collective-permute-start | bytes 12296 | tf_op jit(solution)/shard_map/ppermute | solution.py:33
  5.7 0.6 copy-done.10
  6.5 0.8 collective-permute-done
  7.5 0.5 collective-permute-start.3
  8.0 0.8 collective-permute-done.2
  8.8 1.8 %collective-permute-done.3 = f32[1,8,1,128]{3,1,2,0:T(8,128)S(1)} collective-permute-done((f32[1,8,1,128]{3,1,2,0:T(8,128)S(1)}, f32[1,8,1,128]{3,1,2,0:T(8,128)S(1)}, u32[]{:S(2)}, u32[]{:S(2)}) %collective-permute-start.3) | collective-permute-done | bytes 4128 | tf_op jit(solution)/shard_map/ppermute | solution.py:33
  10.8 0.7 copy-done.6
  12.8 2.0 %collective-permute-start.4 = (f32[1,1,8,128]{3,1,2,0:T(1,128)S(1)}, f32[1,1,8,128]{3,1,2,0:T(1,128)S(1)}, u32[]{:S(2)}, u32[]{:S(2)}) collective-permute-start(f32[1,1,8,128]{3,1,2,0:T(1,128)S(1)} %get-tuple-element.61), channel_id=1, source_target_pairs={{4,0},{8,4},{12,8},{16,12},{20,16},{24,20},{28,24},{0,28},{5,1},{9... | collective-permute-start | bytes 12296 | tf_op jit(solution)/shard_map/ppermute | solution.py:34
  14.8 1.1 collective-permute-start.5
  15.9 1.5 collective-permute-done.4
  17.4 1.1 collective-permute-done.5
  18.7 0.5 collective-permute-start.7
  19.2 0.8 collective-permute-done.6
  20.0 1.8 %collective-permute-done.7 = f32[1,8,1,128]{3,1,2,0:T(8,128)S(1)} collective-permute-done((f32[1,8,1,128]{3,1,2,0:T(8,128)S(1)}, f32[1,8,1,128]{3,1,2,0:T(8,128)S(1)}, u32[]{:S(2)}, u32[]{:S(2)}) %collective-permute-start.7) | collective-permute-done | bytes 4128 | tf_op jit(solution)/shard_map/ppermute | solution.py:33
  23.4 4.8 %collective-permute-start.8 = (f32[1,1,8,128]{3,1,2,0:T(1,128)S(1)}, f32[1,1,8,128]{3,1,2,0:T(1,128)S(1)}, u32[]{:S(2)}, u32[]{:S(2)}) collective-permute-start(f32[1,1,8,128]{3,1,2,0:T(1,128)S(1)} %get-tuple-element.53), channel_id=1, source_target_pairs={{4,0},{8,4},{12,8},{16,12},{20,16},{24,20},{28,24},{0,28},{5,1},{9... | collective-permute-start | bytes 12296 | tf_op jit(solution)/shard_map/ppermute | solution.py:34
  28.2 1.2 collective-permute-done.8
  29.5 2.3 %collective-permute-done.9 = f32[1,1,8,128]{3,1,2,0:T(1,128)S(1)} collective-permute-done((f32[1,1,8,128]{3,1,2,0:T(1,128)S(1)}, f32[1,1,8,128]{3,1,2,0:T(1,128)S(1)}, u32[]{:S(2)}, u32[]{:S(2)}) %collective-permute-start.9) | collective-permute-done | bytes 4128 | tf_op jit(solution)/shard_map/ppermute | solution.py:33
  32.6 0.7 collective-permute-done.10
  33.3 1.8 %collective-permute-done.11 = f32[1,8,1,128]{3,1,2,0:T(8,128)S(1)} collective-permute-done((f32[1,8,1,128]{3,1,2,0:T(8,128)S(1)}, f32[1,8,1,128]{3,1,2,0:T(8,128)S(1)}, u32[]{:S(2)}, u32[]{:S(2)}) %collective-permute-start.11) | collective-permute-done | bytes 4128 | tf_op jit(solution)/shard_map/ppermute | solution.py:33
  35.4 0.5 copy-done.8
  36.4 0.6 copy-done.11
  37.3 3.0 %collective-permute-start.12 = (f32[2,1,8,128]{3,1,2,0:T(1,128)S(1)}, f32[2,1,8,128]{3,1,2,0:T(1,128)S(1)}, u32[]{:S(2)}, u32[]{:S(2)}) collective-permute-start(f32[2,1,8,128]{3,1,2,0:T(1,128)S(1)} %get-tuple-element.29), channel_id=1, source_target_pairs={{4,0},{8,4},{12,8},{16,12},{20,16},{24,20},{28,24},{0,28},{5,1},{9... | collective-permute-start | bytes 24584 | tf_op jit(solution)/shard_map/ppermute | solution.py:34
  40.3 1.6 collective-permute-done.12
  41.9 2.0 %collective-permute-done.13 = f32[2,1,8,128]{3,1,2,0:T(1,128)S(1)} collective-permute-done((f32[2,1,8,128]{3,1,2,0:T(1,128)S(1)}, f32[2,1,8,128]{3,1,2,0:T(1,128)S(1)}, u32[]{:S(2)}, u32[]{:S(2)}) %collective-permute-start.13) | collective-permute-done | bytes 8224 | tf_op jit(solution)/shard_map/ppermute | solution.py:33
  44.1 0.5 collective-permute-start.15
  44.6 0.9 collective-permute-done.14
  45.4 1.8 %collective-permute-done.15 = f32[2,8,1,128]{3,1,2,0:T(8,128)S(1)} collective-permute-done((f32[2,8,1,128]{3,1,2,0:T(8,128)S(1)}, f32[2,8,1,128]{3,1,2,0:T(8,128)S(1)}, u32[]{:S(2)}, u32[]{:S(2)}) %collective-permute-start.15) | collective-permute-done | bytes 8224 | tf_op jit(solution)/shard_map/ppermute | solution.py:33
  48.3 0.6 copy-done.4
  49.3 0.7 copy-done.3
  50.2 2.8 %collective-permute-start.16 = (f32[1,1,8,128]{3,1,2,0:T(1,128)S(1)}, f32[1,1,8,128]{3,1,2,0:T(1,128)S(1)}, u32[]{:S(2)}, u32[]{:S(2)}) collective-permute-start(f32[1,1,8,128]{3,1,2,0:T(1,128)S(1)} %get-tuple-element.45), channel_id=1, source_target_pairs={{4,0},{8,4},{12,8},{16,12},{20,16},{24,20},{28,24},{0,28},{5,1},{9... | collective-permute-start | bytes 12296 | tf_op jit(solution)/shard_map/ppermute | solution.py:34
  53.2 1.6 collective-permute-done.16
  54.7 1.9 %collective-permute-done.17 = f32[1,1,8,128]{3,1,2,0:T(1,128)S(1)} collective-permute-done((f32[1,1,8,128]{3,1,2,0:T(1,128)S(1)}, f32[1,1,8,128]{3,1,2,0:T(1,128)S(1)}, u32[]{:S(2)}, u32[]{:S(2)}) %collective-permute-start.17) | collective-permute-done | bytes 4128 | tf_op jit(solution)/shard_map/ppermute | solution.py:33
  57.3 0.8 collective-permute-done.18
  58.1 1.8 %collective-permute-done.19 = f32[1,8,1,128]{3,1,2,0:T(8,128)S(1)} collective-permute-done((f32[1,8,1,128]{3,1,2,0:T(8,128)S(1)}, f32[1,8,1,128]{3,1,2,0:T(8,128)S(1)}, u32[]{:S(2)}, u32[]{:S(2)}) %collective-permute-start.19) | collective-permute-done | bytes 4128 | tf_op jit(solution)/shard_map/ppermute | solution.py:33
  60.1 0.7 fusion.105
  60.8 44.3 %all-reduce.1 = (f32[]{:T(128)}, f32[]{:T(128)}) all-reduce(f32[]{:T(128)} %get-tuple-element.9, f32[]{:T(128)} %get-tuple-element.8), channel_id=1, replica_groups=mesh['dom'=8,'sub'=4] {'dom','sub'}, use_global_device_ids=true, to_apply=%region_1.2 | all-reduce | flops 2 | bytes 16 | tf_op jit(solution)/shard_map/psum | solution.py:135
  107.7 0.6 collective-permute-start.20
  108.4 2.3 %collective-permute-start.21 = (f32[1,1,8,128]{3,1,2,0:T(1,128)S(1)}, f32[1,1,8,128]{3,1,2,0:T(1,128)S(1)}, u32[]{:S(2)}, u32[]{:S(2)}) collective-permute-start(f32[1,1,8,128]{3,1,2,0:T(1,128)S(1)} %get-tuple-element.38), channel_id=1, source_target_pairs={{0,4},{4,8},{8,12},{12,16},{16,20},{20,24},{24,28},{28,0},{1,5},{5... | collective-permute-start | bytes 12296 | tf_op jit(solution)/shard_map/ppermute | solution.py:33
  110.7 1.6 collective-permute-done.20
  113.0 0.6 copy.103
  113.8 1.8 %collective-permute-done.23 = f32[1,8,1,128]{3,1,2,0:T(8,128)S(1)} collective-permute-done((f32[1,8,1,128]{3,1,2,0:T(8,128)S(1)}, f32[1,8,1,128]{3,1,2,0:T(8,128)S(1)}, u32[]{:S(2)}, u32[]{:S(2)}) %collective-permute-start.23) | collective-permute-done | bytes 4128 | tf_op jit(solution)/shard_map/ppermute | solution.py:33
  115.8 0.8 fusion.107
  116.6 43.1 %all-reduce = (f32[]{:T(128)}, f32[]{:T(128)}) all-reduce(f32[]{:T(128)} %get-tuple-element.7, f32[]{:T(128)} %get-tuple-element.6), channel_id=1, replica_groups=mesh['dom'=8,'sub'=4] {'dom','sub'}, use_global_device_ids=true, to_apply=%region_5.6 | all-reduce | flops 2 | bytes 16 | tf_op jit(solution)/shard_map/psum | solution.py:135
  164.3 0.6 copy.105
  164.9 0.6 copy.104
  (120 shorter events, 11.2 us)
Async XLA Ops:
  0.6 0.8 copy-start.1
  0.6 0.8 copy-start.2
  1.6 0.9 copy-start
  2.8 4.6 %collective-permute-start = (f32[1,1,8,128]{3,1,2,0:T(1,128)S(1)}, f32[1,1,8,128]{3,1,2,0:T(1,128)S(1)}, u32[]{:S(2)}, u32[]{:S(2)}) collective-permute-start(f32[1,1,8,128]{3,1,2,0:T(1,128)S(1)} %get-tuple-element.73), channel_id=1, source_target_pairs={{4,0},{8,4},{12,8},{16,12},{20,16},{24,20},{28,24},{0,28},{5,1},{9... | collective-permute-start | bytes 12296 | tf_op jit(solution)/shard_map/ppermute | solution.py:34
  3.3 4.0 %collective-permute-start.1 = (f32[1,1,8,128]{3,1,2,0:T(1,128)S(1)}, f32[1,1,8,128]{3,1,2,0:T(1,128)S(1)}, u32[]{:S(2)}, u32[]{:S(2)}) collective-permute-start(f32[1,1,8,128]{3,1,2,0:T(1,128)S(1)} %get-tuple-element.74), channel_id=1, source_target_pairs={{0,4},{4,8},{8,12},{12,16},{16,20},{20,24},{24,28},{28,0},{1,5},{5... | collective-permute-start | bytes 12296 | tf_op jit(solution)/shard_map/ppermute | solution.py:33
  5.7 0.7 copy-start.10
  7.4 1.4 collective-permute-start.2
  7.5 3.1 %collective-permute-start.3 = (f32[1,8,1,128]{3,1,2,0:T(8,128)S(1)}, f32[1,8,1,128]{3,1,2,0:T(8,128)S(1)}, u32[]{:S(2)}, u32[]{:S(2)}) collective-permute-start(f32[1,8,1,128]{3,1,2,0:T(8,128)S(1)} %get-tuple-element.72), channel_id=1, source_target_pairs={{0,1},{1,2},{2,3},{3,0},{4,5},{5,6},{6,7},{7,4},{8,9},{9,10},{10,1... | collective-permute-start | bytes 12296 | tf_op jit(solution)/shard_map/ppermute | solution.py:33
  10.8 0.7 copy-start.6
  12.8 4.6 %collective-permute-start.4 = (f32[1,1,8,128]{3,1,2,0:T(1,128)S(1)}, f32[1,1,8,128]{3,1,2,0:T(1,128)S(1)}, u32[]{:S(2)}, u32[]{:S(2)}) collective-permute-start(f32[1,1,8,128]{3,1,2,0:T(1,128)S(1)} %get-tuple-element.61), channel_id=1, source_target_pairs={{4,0},{8,4},{12,8},{16,12},{20,16},{24,20},{28,24},{0,28},{5,1},{9... | collective-permute-start | bytes 12296 | tf_op jit(solution)/shard_map/ppermute | solution.py:34
  14.8 3.7 %collective-permute-start.5 = (f32[1,1,8,128]{3,1,2,0:T(1,128)S(1)}, f32[1,1,8,128]{3,1,2,0:T(1,128)S(1)}, u32[]{:S(2)}, u32[]{:S(2)}) collective-permute-start(f32[1,1,8,128]{3,1,2,0:T(1,128)S(1)} %get-tuple-element.62), channel_id=1, source_target_pairs={{0,4},{4,8},{8,12},{12,16},{16,20},{20,24},{24,28},{28,0},{1,5},{5... | collective-permute-start | bytes 12296 | tf_op jit(solution)/shard_map/ppermute | solution.py:33
  18.6 1.4 collective-permute-start.6
  18.7 3.1 %collective-permute-start.7 = (f32[1,8,1,128]{3,1,2,0:T(8,128)S(1)}, f32[1,8,1,128]{3,1,2,0:T(8,128)S(1)}, u32[]{:S(2)}, u32[]{:S(2)}) collective-permute-start(f32[1,8,1,128]{3,1,2,0:T(8,128)S(1)} %get-tuple-element.60), channel_id=1, source_target_pairs={{0,1},{1,2},{2,3},{3,0},{4,5},{5,6},{6,7},{7,4},{8,9},{9,10},{10,1... | collective-permute-start | bytes 12296 | tf_op jit(solution)/shard_map/ppermute | solution.py:33
  23.4 4.8 %copy-start.9 = (f32[8]{0:T(128)S(1)}, f32[8]{0:T(128)}, u32[]{:S(2)}) copy-start(f32[8]{0:T(128)} %constant.109.clone) | copy-start | bytes 100
  23.4 6.1 %collective-permute-start.8 = (f32[1,1,8,128]{3,1,2,0:T(1,128)S(1)}, f32[1,1,8,128]{3,1,2,0:T(1,128)S(1)}, u32[]{:S(2)}, u32[]{:S(2)}) collective-permute-start(f32[1,1,8,128]{3,1,2,0:T(1,128)S(1)} %get-tuple-element.53), channel_id=1, source_target_pairs={{4,0},{8,4},{12,8},{16,12},{20,16},{24,20},{28,24},{0,28},{5,1},{9... | collective-permute-start | bytes 12296 | tf_op jit(solution)/shard_map/ppermute | solution.py:34
  28.2 3.6 %collective-permute-start.9 = (f32[1,1,8,128]{3,1,2,0:T(1,128)S(1)}, f32[1,1,8,128]{3,1,2,0:T(1,128)S(1)}, u32[]{:S(2)}, u32[]{:S(2)}) collective-permute-start(f32[1,1,8,128]{3,1,2,0:T(1,128)S(1)} %get-tuple-element.54), channel_id=1, source_target_pairs={{0,4},{4,8},{8,12},{12,16},{16,20},{20,24},{24,28},{28,0},{1,5},{5... | collective-permute-start | bytes 12296 | tf_op jit(solution)/shard_map/ppermute | solution.py:33
  28.2 4.2 %copy-start.5 = (f32[8,8,128]{2,1,0:T(8,128)S(1)}, f32[8,8,128]{2,1,0:T(8,128)}, u32[]{:S(2)}) copy-start(f32[8,8,128]{2,1,0:T(8,128)} %param.41) | copy-start | bytes 98308
  31.9 0.7 copy-start.7
  31.9 1.4 collective-permute-start.10
  31.9 3.1 %collective-permute-start.11 = (f32[1,8,1,128]{3,1,2,0:T(8,128)S(1)}, f32[1,8,1,128]{3,1,2,0:T(8,128)S(1)}, u32[]{:S(2)}, u32[]{:S(2)}) collective-permute-start(f32[1,8,1,128]{3,1,2,0:T(8,128)S(1)} %get-tuple-element.52), channel_id=1, source_target_pairs={{0,1},{1,2},{2,3},{3,0},{4,5},{5,6},{6,7},{7,4},{8,9},{9,10},{10,1... | collective-permute-start | bytes 12296 | tf_op jit(solution)/shard_map/ppermute | solution.py:33
  35.3 0.7 copy-start.8
  36.1 0.9 copy-start.11
  37.3 4.6 %collective-permute-start.12 = (f32[2,1,8,128]{3,1,2,0:T(1,128)S(1)}, f32[2,1,8,128]{3,1,2,0:T(1,128)S(1)}, u32[]{:S(2)}, u32[]{:S(2)}) collective-permute-start(f32[2,1,8,128]{3,1,2,0:T(1,128)S(1)} %get-tuple-element.29), channel_id=1, source_target_pairs={{4,0},{8,4},{12,8},{16,12},{20,16},{24,20},{28,24},{0,28},{5,1},{9... | collective-permute-start | bytes 24584 | tf_op jit(solution)/shard_map/ppermute | solution.py:34
  40.3 3.7 %collective-permute-start.13 = (f32[2,1,8,128]{3,1,2,0:T(1,128)S(1)}, f32[2,1,8,128]{3,1,2,0:T(1,128)S(1)}, u32[]{:S(2)}, u32[]{:S(2)}) collective-permute-start(f32[2,1,8,128]{3,1,2,0:T(1,128)S(1)} %get-tuple-element.30), channel_id=1, source_target_pairs={{0,4},{4,8},{8,12},{12,16},{16,20},{20,24},{24,28},{28,0},{1,5},{5... | collective-permute-start | bytes 24584 | tf_op jit(solution)/shard_map/ppermute | solution.py:33
  44.0 1.4 collective-permute-start.14
  44.1 3.1 %collective-permute-start.15 = (f32[2,8,1,128]{3,1,2,0:T(8,128)S(1)}, f32[2,8,1,128]{3,1,2,0:T(8,128)S(1)}, u32[]{:S(2)}, u32[]{:S(2)}) collective-permute-start(f32[2,8,1,128]{3,1,2,0:T(8,128)S(1)} %get-tuple-element.28), channel_id=1, source_target_pairs={{0,1},{1,2},{2,3},{3,0},{4,5},{5,6},{6,7},{7,4},{8,9},{9,10},{10,1... | collective-permute-start | bytes 24584 | tf_op jit(solution)/shard_map/ppermute | solution.py:33
  48.2 0.7 copy-start.4
  49.1 0.8 copy-start.3
  50.2 4.6 %collective-permute-start.16 = (f32[1,1,8,128]{3,1,2,0:T(1,128)S(1)}, f32[1,1,8,128]{3,1,2,0:T(1,128)S(1)}, u32[]{:S(2)}, u32[]{:S(2)}) collective-permute-start(f32[1,1,8,128]{3,1,2,0:T(1,128)S(1)} %get-tuple-element.45), channel_id=1, source_target_pairs={{4,0},{8,4},{12,8},{16,12},{20,16},{24,20},{28,24},{0,28},{5,1},{9... | collective-permute-start | bytes 12296 | tf_op jit(solution)/shard_map/ppermute | solution.py:34
  53.0 3.6 %collective-permute-start.17 = (f32[1,1,8,128]{3,1,2,0:T(1,128)S(1)}, f32[1,1,8,128]{3,1,2,0:T(1,128)S(1)}, u32[]{:S(2)}, u32[]{:S(2)}) collective-permute-start(f32[1,1,8,128]{3,1,2,0:T(1,128)S(1)} %get-tuple-element.46), channel_id=1, source_target_pairs={{0,4},{4,8},{8,12},{12,16},{16,20},{20,24},{24,28},{28,0},{1,5},{5... | collective-permute-start | bytes 12296 | tf_op jit(solution)/shard_map/ppermute | solution.py:33
  56.7 1.4 collective-permute-start.18
  56.8 3.1 %collective-permute-start.19 = (f32[1,8,1,128]{3,1,2,0:T(8,128)S(1)}, f32[1,8,1,128]{3,1,2,0:T(8,128)S(1)}, u32[]{:S(2)}, u32[]{:S(2)}) collective-permute-start(f32[1,8,1,128]{3,1,2,0:T(8,128)S(1)} %get-tuple-element.44), channel_id=1, source_target_pairs={{0,1},{1,2},{2,3},{3,0},{4,5},{5,6},{6,7},{7,4},{8,9},{9,10},{10,1... | collective-permute-start | bytes 12296 | tf_op jit(solution)/shard_map/ppermute | solution.py:33
  107.7 4.6 %collective-permute-start.20 = (f32[1,1,8,128]{3,1,2,0:T(1,128)S(1)}, f32[1,1,8,128]{3,1,2,0:T(1,128)S(1)}, u32[]{:S(2)}, u32[]{:S(2)}) collective-permute-start(f32[1,1,8,128]{3,1,2,0:T(1,128)S(1)} %get-tuple-element.37), channel_id=1, source_target_pairs={{4,0},{8,4},{12,8},{16,12},{20,16},{24,20},{28,24},{0,28},{5,1},{9... | collective-permute-start | bytes 12296 | tf_op jit(solution)/shard_map/ppermute | solution.py:34
  108.4 3.9 %collective-permute-start.21 = (f32[1,1,8,128]{3,1,2,0:T(1,128)S(1)}, f32[1,1,8,128]{3,1,2,0:T(1,128)S(1)}, u32[]{:S(2)}, u32[]{:S(2)}) collective-permute-start(f32[1,1,8,128]{3,1,2,0:T(1,128)S(1)} %get-tuple-element.38), channel_id=1, source_target_pairs={{0,4},{4,8},{8,12},{12,16},{16,20},{20,24},{24,28},{28,0},{1,5},{5... | collective-permute-start | bytes 12296 | tf_op jit(solution)/shard_map/ppermute | solution.py:33
  112.4 1.4 collective-permute-start.22
  112.5 3.1 %collective-permute-start.23 = (f32[1,8,1,128]{3,1,2,0:T(8,128)S(1)}, f32[1,8,1,128]{3,1,2,0:T(8,128)S(1)}, u32[]{:S(2)}, u32[]{:S(2)}) collective-permute-start(f32[1,8,1,128]{3,1,2,0:T(8,128)S(1)} %get-tuple-element.36), channel_id=1, source_target_pairs={{0,1},{1,2},{2,3},{3,0},{4,5},{5,6},{6,7},{7,4},{8,9},{9,10},{10,1... | collective-permute-start | bytes 12296 | tf_op jit(solution)/shard_map/ppermute | solution.py:33
where the time goes:
time: 166 us
  blocking collectives  87.4 us (53%)
  waiting for transfers between devices  30.5 us (18%)
  starting transfers between devices  23.1 us (14%)
  local copies, waits for them, and re-layouts  8.16 us (5%)
  between operations  7.03 us (4%)
  matrix products  5.75 us (3%)
  other arithmetic  3.65 us (2%)
    psum x2, blocking collectives, both_sums(): lax.psum((jnp.sum(residual * precond * inv_mult), jnp.sum(precond * appli...  87.4 us
    ppermute x12, waiting for transfers between devices, padded(): before = lax.ppermute(last, axis, up)  17.9 us
    ppermute x12, starting transfers between devices, padded(): after = lax.ppermute(leading, axis, down)  14.1 us
    ppermute x12, waiting for transfers between devices, padded(): after = lax.ppermute(leading, axis, down)  12.6 us
    ppermute x12, starting transfers between devices, padded(): before = lax.ppermute(last, axis, up)  8.96 us
    unnamed x27, local copies, waits for them, and re-layouts  6.39 us
  transfers between devices with their start and end apart: 24, of which 22 were waited for; matrix products, arithmetic and copies ran while one was open for 1% of the time, Pallas kernels for 0%

commit v1 on v0

--- a/solution.py
+++ b/solution.py
@@ -21,6 +21,10 @@
 reinit_step = 0.02
 interface_width = 0.1
 density_ratio = 9.0
+
+
+def _use_tasks(field_in):
+    return jax.lax.psum(jax.lax.psum(field_in, "dom"), "sub")
 
 
 def padded(x, sides, width):
@@ -132,9 +136,8 @@
 
 
 def both_sums(residual, precond, applied, inv_mult):
-    return lax.psum(
-        (jnp.sum(residual * precond * inv_mult), jnp.sum(precond * applied * inv_mult)),
-        ("dom", "sub"),
+    return _use_tasks(
+        (jnp.sum(residual * precond * inv_mult), jnp.sum(precond * applied * inv_mult))
     )
 
 

time: 166 us -> 137 us (0.83)
  the two profiles are of different devices: /device:TPU:14 before, /device:TPU:0 now
where the time goes in v1:
time: 137 us
  blocking collectives  48.2 us (35%)
  waiting for transfers between devices  44.1 us (32%)
  starting transfers between devices  19.8 us (14%)
  local copies, waits for them, and re-layouts  8.15 us (6%)
  between operations  7.11 us (5%)
  matrix products  5.75 us (4%)
  other arithmetic  3.64 us (3%)
    psum x4, blocking collectives, _use_tasks(): return jax.lax.psum(jax.lax.psum(field_in, 'dom'), 'sub')  48.2 us
    ppermute x12, waiting for transfers between devices, padded(): before = lax.ppermute(last, axis, up)  31.5 us
    ppermute x12, waiting for transfers between devices, padded(): after = lax.ppermute(leading, axis, down)  12.6 us
    ppermute x12, starting transfers between devices, padded(): before = lax.ppermute(last, axis, up)  11.1 us
    ppermute x12, starting transfers between devices, padded(): after = lax.ppermute(leading, axis, down)  8.7 us
    unnamed x27, local copies, waits for them, and re-layouts  6.38 us
  transfers between devices with their start and end apart: 24, of which 24 were waited for; matrix products, arithmetic and copies ran while one was open for 1% of the time, Pallas kernels for 0%

profile of v1, /device:TPU:0, one launch (start us, length us, event | category | flops | bytes accessed | tf_op | source)
XLA Modules:
  0.0 136.7 jit_solution(9894822514776414924)
XLA Ops:
  0.7 0.8 fusion.168
  1.8 0.7 copy-done
  2.7 6.1 %collective-permute-start = (f32[1,1,8,128]{3,1,2,0:T(1,128)S(1)}, f32[1,1,8,128]{3,1,2,0:T(1,128)S(1)}, u32[]{:S(2)}, u32[]{:S(2)}) collective-permute-start(f32[1,1,8,128]{3,1,2,0:T(1,128)S(1)} %get-tuple-element.77), channel_id=1, source_target_pairs={{4,0},{8,4},{12,8},{16,12},{20,16},{24,20},{28,24},{0,28},{5,1},{9... | collective-permute-start | bytes 12296 | tf_op jit(solution)/shard_map/ppermute | solution.py:38
  8.8 0.6 copy-done.10
  9.6 0.6 collective-permute-done
  10.1 5.0 %collective-permute-done.1 = f32[1,1,8,128]{3,1,2,0:T(1,128)S(1)} collective-permute-done((f32[1,1,8,128]{3,1,2,0:T(1,128)S(1)}, f32[1,1,8,128]{3,1,2,0:T(1,128)S(1)}, u32[]{:S(2)}, u32[]{:S(2)}) %collective-permute-start.1) | collective-permute-done | bytes 4128 | tf_op jit(solution)/shard_map/ppermute | solution.py:37
  15.8 0.8 collective-permute-done.2
  16.6 1.8 %collective-permute-done.3 = f32[1,8,1,128]{3,1,2,0:T(8,128)S(1)} collective-permute-done((f32[1,8,1,128]{3,1,2,0:T(8,128)S(1)}, f32[1,8,1,128]{3,1,2,0:T(8,128)S(1)}, u32[]{:S(2)}, u32[]{:S(2)}) %collective-permute-start.3) | collective-permute-done | bytes 4128 | tf_op jit(solution)/shard_map/ppermute | solution.py:37
  18.6 0.7 copy-done.6
  20.7 2.0 %collective-permute-start.5 = (f32[1,1,8,128]{3,1,2,0:T(1,128)S(1)}, f32[1,1,8,128]{3,1,2,0:T(1,128)S(1)}, u32[]{:S(2)}, u32[]{:S(2)}) collective-permute-start(f32[1,1,8,128]{3,1,2,0:T(1,128)S(1)} %get-tuple-element.66), channel_id=1, source_target_pairs={{0,4},{4,8},{8,12},{12,16},{16,20},{20,24},{24,28},{28,0},{1,5},{5... | collective-permute-start | bytes 12296 | tf_op jit(solution)/shard_map/ppermute | solution.py:37
  22.8 1.6 %collective-permute-done.4 = f32[1,1,8,128]{3,1,2,0:T(1,128)S(1)} collective-permute-done((f32[1,1,8,128]{3,1,2,0:T(1,128)S(1)}, f32[1,1,8,128]{3,1,2,0:T(1,128)S(1)}, u32[]{:S(2)}, u32[]{:S(2)}) %collective-permute-start.4) | collective-permute-done | bytes 4128 | tf_op jit(solution)/shard_map/ppermute | solution.py:38
  24.3 2.8 %collective-permute-done.5 = f32[1,1,8,128]{3,1,2,0:T(1,128)S(1)} collective-permute-done((f32[1,1,8,128]{3,1,2,0:T(1,128)S(1)}, f32[1,1,8,128]{3,1,2,0:T(1,128)S(1)}, u32[]{:S(2)}, u32[]{:S(2)}) %collective-permute-start.5) | collective-permute-done | bytes 4128 | tf_op jit(solution)/shard_map/ppermute | solution.py:37
  27.3 0.5 collective-permute-start.7
  27.7 0.8 collective-permute-done.6
  28.6 1.8 %collective-permute-done.7 = f32[1,8,1,128]{3,1,2,0:T(8,128)S(1)} collective-permute-done((f32[1,8,1,128]{3,1,2,0:T(8,128)S(1)}, f32[1,8,1,128]{3,1,2,0:T(8,128)S(1)}, u32[]{:S(2)}, u32[]{:S(2)}) %collective-permute-start.7) | collective-permute-done | bytes 4128 | tf_op jit(solution)/shard_map/ppermute | solution.py:37
  32.1 2.0 %collective-permute-start.9 = (f32[1,1,8,128]{3,1,2,0:T(1,128)S(1)}, f32[1,1,8,128]{3,1,2,0:T(1,128)S(1)}, u32[]{:S(2)}, u32[]{:S(2)}) collective-permute-start(f32[1,1,8,128]{3,1,2,0:T(1,128)S(1)} %get-tuple-element.58), channel_id=1, source_target_pairs={{0,4},{4,8},{8,12},{12,16},{16,20},{20,24},{24,28},{28,0},{1,5},{5... | collective-permute-start | bytes 12296 | tf_op jit(solution)/shard_map/ppermute | solution.py:37
  34.1 1.5 %collective-permute-done.8 = f32[1,1,8,128]{3,1,2,0:T(1,128)S(1)} collective-permute-done((f32[1,1,8,128]{3,1,2,0:T(1,128)S(1)}, f32[1,1,8,128]{3,1,2,0:T(1,128)S(1)}, u32[]{:S(2)}, u32[]{:S(2)}) %collective-permute-start.8) | collective-permute-done | bytes 4128 | tf_op jit(solution)/shard_map/ppermute | solution.py:38
  35.6 2.8 %collective-permute-done.9 = f32[1,1,8,128]{3,1,2,0:T(1,128)S(1)} collective-permute-done((f32[1,1,8,128]{3,1,2,0:T(1,128)S(1)}, f32[1,1,8,128]{3,1,2,0:T(1,128)S(1)}, u32[]{:S(2)}, u32[]{:S(2)}) %collective-permute-start.9) | collective-permute-done | bytes 4128 | tf_op jit(solution)/shard_map/ppermute | solution.py:37
  39.2 0.7 collective-permute-done.10
  39.9 1.8 %collective-permute-done.11 = f32[1,8,1,128]{3,1,2,0:T(8,128)S(1)} collective-permute-done((f32[1,8,1,128]{3,1,2,0:T(8,128)S(1)}, f32[1,8,1,128]{3,1,2,0:T(8,128)S(1)}, u32[]{:S(2)}, u32[]{:S(2)}) %collective-permute-start.11) | collective-permute-done | bytes 4128 | tf_op jit(solution)/shard_map/ppermute | solution.py:37
  42.1 0.5 copy-done.8
  43.0 0.6 copy-done.11
  44.0 2.0 %collective-permute-start.13 = (f32[2,1,8,128]{3,1,2,0:T(1,128)S(1)}, f32[2,1,8,128]{3,1,2,0:T(1,128)S(1)}, u32[]{:S(2)}, u32[]{:S(2)}) collective-permute-start(f32[2,1,8,128]{3,1,2,0:T(1,128)S(1)} %get-tuple-element.34), channel_id=1, source_target_pairs={{0,4},{4,8},{8,12},{12,16},{16,20},{20,24},{24,28},{28,0},{1,5},{5... | collective-permute-start | bytes 24584 | tf_op jit(solution)/shard_map/ppermute | solution.py:37
  46.0 1.6 %collective-permute-done.12 = f32[2,1,8,128]{3,1,2,0:T(1,128)S(1)} collective-permute-done((f32[2,1,8,128]{3,1,2,0:T(1,128)S(1)}, f32[2,1,8,128]{3,1,2,0:T(1,128)S(1)}, u32[]{:S(2)}, u32[]{:S(2)}) %collective-permute-start.12) | collective-permute-done | bytes 8224 | tf_op jit(solution)/shard_map/ppermute | solution.py:38
  47.6 2.8 %collective-permute-done.13 = f32[2,1,8,128]{3,1,2,0:T(1,128)S(1)} collective-permute-done((f32[2,1,8,128]{3,1,2,0:T(1,128)S(1)}, f32[2,1,8,128]{3,1,2,0:T(1,128)S(1)}, u32[]{:S(2)}, u32[]{:S(2)}) %collective-permute-start.13) | collective-permute-done | bytes 8224 | tf_op jit(solution)/shard_map/ppermute | solution.py:37
  51.0 0.9 collective-permute-done.14
  51.9 1.8 %collective-permute-done.15 = f32[2,8,1,128]{3,1,2,0:T(8,128)S(1)} collective-permute-done((f32[2,8,1,128]{3,1,2,0:T(8,128)S(1)}, f32[2,8,1,128]{3,1,2,0:T(8,128)S(1)}, u32[]{:S(2)}, u32[]{:S(2)}) %collective-permute-start.15) | collective-permute-done | bytes 8224 | tf_op jit(solution)/shard_map/ppermute | solution.py:37
  54.8 0.6 copy-done.4
  55.8 0.7 copy-done.3
  56.8 2.0 %collective-permute-start.17 = (f32[1,1,8,128]{3,1,2,0:T(1,128)S(1)}, f32[1,1,8,128]{3,1,2,0:T(1,128)S(1)}, u32[]{:S(2)}, u32[]{:S(2)}) collective-permute-start(f32[1,1,8,128]{3,1,2,0:T(1,128)S(1)} %get-tuple-element.50), channel_id=1, source_target_pairs={{0,4},{4,8},{8,12},{12,16},{16,20},{20,24},{24,28},{28,0},{1,5},{5... | collective-permute-start | bytes 12296 | tf_op jit(solution)/shard_map/ppermute | solution.py:37
  58.8 1.6 %collective-permute-done.16 = f32[1,1,8,128]{3,1,2,0:T(1,128)S(1)} collective-permute-done((f32[1,1,8,128]{3,1,2,0:T(1,128)S(1)}, f32[1,1,8,128]{3,1,2,0:T(1,128)S(1)}, u32[]{:S(2)}, u32[]{:S(2)}) %collective-permute-start.16) | collective-permute-done | bytes 4128 | tf_op jit(solution)/shard_map/ppermute | solution.py:38
  60.4 2.8 %collective-permute-done.17 = f32[1,1,8,128]{3,1,2,0:T(1,128)S(1)} collective-permute-done((f32[1,1,8,128]{3,1,2,0:T(1,128)S(1)}, f32[1,1,8,128]{3,1,2,0:T(1,128)S(1)}, u32[]{:S(2)}, u32[]{:S(2)}) %collective-permute-start.17) | collective-permute-done | bytes 4128 | tf_op jit(solution)/shard_map/ppermute | solution.py:37
  63.8 0.8 collective-permute-done.18
  64.6 1.8 %collective-permute-done.19 = f32[1,8,1,128]{3,1,2,0:T(8,128)S(1)} collective-permute-done((f32[1,8,1,128]{3,1,2,0:T(8,128)S(1)}, f32[1,8,1,128]{3,1,2,0:T(8,128)S(1)}, u32[]{:S(2)}, u32[]{:S(2)}) %collective-permute-start.19) | collective-permute-done | bytes 4128 | tf_op jit(solution)/shard_map/ppermute | solution.py:37
  66.6 0.7 fusion.105
  67.3 17.8 %all-reduce.1 = (f32[]{:T(128)}, f32[]{:T(128)}) all-reduce(f32[]{:T(128)} %get-tuple-element.9, f32[]{:T(128)} %get-tuple-element.8), channel_id=1, replica_groups=mesh['dom'=8,'sub'=4] {'dom'}, use_global_device_ids=true, to_apply=%region_1.2 | all-reduce | flops 2 | bytes 16 | tf_op jit(solution)/shard_map/psum | solution.py:27
  85.1 6.3 %all-reduce.3 = (f32[]{:T(128)}, f32[]{:T(128)}) all-reduce(f32[]{:T(128)} %get-tuple-element.12, f32[]{:T(128)} %get-tuple-element.13), channel_id=1, replica_groups=mesh['dom'=8,'sub'=4] {'sub'}, use_global_device_ids=true, to_apply=%region_2.3 | all-reduce | flops 2 | bytes 16 | tf_op jit(solution)/shard_map/psum | solution.py:27
  94.0 2.1 %collective-permute-start.20 = (f32[1,1,8,128]{3,1,2,0:T(1,128)S(1)}, f32[1,1,8,128]{3,1,2,0:T(1,128)S(1)}, u32[]{:S(2)}, u32[]{:S(2)}) collective-permute-start(f32[1,1,8,128]{3,1,2,0:T(1,128)S(1)} %get-tuple-element.41), channel_id=1, source_target_pairs={{4,0},{8,4},{12,8},{16,12},{20,16},{24,20},{28,24},{0,28},{5,1},{9... | collective-permute-start | bytes 12296 | tf_op jit(solution)/shard_map/ppermute | solution.py:38
  96.1 1.5 %collective-permute-done.20 = f32[1,1,8,128]{3,1,2,0:T(1,128)S(1)} collective-permute-done((f32[1,1,8,128]{3,1,2,0:T(1,128)S(1)}, f32[1,1,8,128]{3,1,2,0:T(1,128)S(1)}, u32[]{:S(2)}, u32[]{:S(2)}) %collective-permute-start.20) | collective-permute-done | bytes 4128 | tf_op jit(solution)/shard_map/ppermute | solution.py:38
  97.7 4.7 %collective-permute-done.21 = f32[1,1,8,128]{3,1,2,0:T(1,128)S(1)} collective-permute-done((f32[1,1,8,128]{3,1,2,0:T(1,128)S(1)}, f32[1,1,8,128]{3,1,2,0:T(1,128)S(1)}, u32[]{:S(2)}, u32[]{:S(2)}) %collective-permute-start.21) | collective-permute-done | bytes 4128 | tf_op jit(solution)/shard_map/ppermute | solution.py:37
  102.5 0.5 collective-permute-start.23
  103.0 0.6 copy.103
  103.8 1.8 %collective-permute-done.23 = f32[1,8,1,128]{3,1,2,0:T(8,128)S(1)} collective-permute-done((f32[1,8,1,128]{3,1,2,0:T(8,128)S(1)}, f32[1,8,1,128]{3,1,2,0:T(8,128)S(1)}, u32[]{:S(2)}, u32[]{:S(2)}) %collective-permute-start.23) | collective-permute-done | bytes 4128 | tf_op jit(solution)/shard_map/ppermute | solution.py:37
  105.9 0.8 fusion.107
  106.7 17.8 %all-reduce = (f32[]{:T(128)}, f32[]{:T(128)}) all-reduce(f32[]{:T(128)} %get-tuple-element.7, f32[]{:T(128)} %get-tuple-element.6), channel_id=1, replica_groups=mesh['dom'=8,'sub'=4] {'dom'}, use_global_device_ids=true, to_apply=%region_7.8 | all-reduce | flops 2 | bytes 16 | tf_op jit(solution)/shard_map/psum | solution.py:27
  124.5 6.3 %all-reduce.2 = (f32[]{:T(128)}, f32[]{:T(128)}) all-reduce(f32[]{:T(128)} %get-tuple-element.10, f32[]{:T(128)} %get-tuple-element.11), channel_id=1, replica_groups=mesh['dom'=8,'sub'=4] {'sub'}, use_global_device_ids=true, to_apply=%region_8.9 | all-reduce | flops 2 | bytes 16 | tf_op jit(solution)/shard_map/psum | solution.py:27
  135.4 0.6 copy.105
  136.1 0.6 copy.104
  (122 shorter events, 11.8 us)
Async XLA Ops:
  0.6 0.8 copy-start.1
  0.6 0.8 copy-start.2
  1.6 0.8 copy-start
  2.7 7.4 %collective-permute-start = (f32[1,1,8,128]{3,1,2,0:T(1,128)S(1)}, f32[1,1,8,128]{3,1,2,0:T(1,128)S(1)}, u32[]{:S(2)}, u32[]{:S(2)}) collective-permute-start(f32[1,1,8,128]{3,1,2,0:T(1,128)S(1)} %get-tuple-element.77), channel_id=1, source_target_pairs={{4,0},{8,4},{12,8},{16,12},{20,16},{24,20},{28,24},{0,28},{5,1},{9... | collective-permute-start | bytes 12296 | tf_op jit(solution)/shard_map/ppermute | solution.py:38
  8.8 6.3 %collective-permute-start.1 = (f32[1,1,8,128]{3,1,2,0:T(1,128)S(1)}, f32[1,1,8,128]{3,1,2,0:T(1,128)S(1)}, u32[]{:S(2)}, u32[]{:S(2)}) collective-permute-start(f32[1,1,8,128]{3,1,2,0:T(1,128)S(1)} %get-tuple-element.78), channel_id=1, source_target_pairs={{0,4},{4,8},{8,12},{12,16},{16,20},{20,24},{24,28},{28,0},{1,5},{5... | collective-permute-start | bytes 12296 | tf_op jit(solution)/shard_map/ppermute | solution.py:37
  8.8 0.7 copy-start.10
  15.2 1.4 %collective-permute-start.2 = (f32[1,8,1,128]{3,1,2,0:T(8,128)S(1)}, f32[1,8,1,128]{3,1,2,0:T(8,128)S(1)}, u32[]{:S(2)}, u32[]{:S(2)}) collective-permute-start(f32[1,8,1,128]{3,1,2,0:T(8,128)S(1)} %get-tuple-element.75), channel_id=1, source_target_pairs={{1,0},{2,1},{3,2},{0,3},{5,4},{6,5},{7,6},{4,7},{9,8},{10,9},{11,1... | collective-permute-start | bytes 12296 | tf_op jit(solution)/shard_map/ppermute | solution.py:38
  15.3 3.1 %collective-permute-start.3 = (f32[1,8,1,128]{3,1,2,0:T(8,128)S(1)}, f32[1,8,1,128]{3,1,2,0:T(8,128)S(1)}, u32[]{:S(2)}, u32[]{:S(2)}) collective-permute-start(f32[1,8,1,128]{3,1,2,0:T(8,128)S(1)} %get-tuple-element.76), channel_id=1, source_target_pairs={{0,1},{1,2},{2,3},{3,0},{4,5},{5,6},{6,7},{7,4},{8,9},{9,10},{10,1... | collective-permute-start | bytes 12296 | tf_op jit(solution)/shard_map/ppermute | solution.py:37
  18.6 0.7 copy-start.6
  20.7 3.7 %collective-permute-start.4 = (f32[1,1,8,128]{3,1,2,0:T(1,128)S(1)}, f32[1,1,8,128]{3,1,2,0:T(1,128)S(1)}, u32[]{:S(2)}, u32[]{:S(2)}) collective-permute-start(f32[1,1,8,128]{3,1,2,0:T(1,128)S(1)} %get-tuple-element.65), channel_id=1, source_target_pairs={{4,0},{8,4},{12,8},{16,12},{20,16},{24,20},{28,24},{0,28},{5,1},{9... | collective-permute-start | bytes 12296 | tf_op jit(solution)/shard_map/ppermute | solution.py:38
  20.7 6.4 %collective-permute-start.5 = (f32[1,1,8,128]{3,1,2,0:T(1,128)S(1)}, f32[1,1,8,128]{3,1,2,0:T(1,128)S(1)}, u32[]{:S(2)}, u32[]{:S(2)}) collective-permute-start(f32[1,1,8,128]{3,1,2,0:T(1,128)S(1)} %get-tuple-element.66), channel_id=1, source_target_pairs={{0,4},{4,8},{8,12},{12,16},{16,20},{20,24},{24,28},{28,0},{1,5},{5... | collective-permute-start | bytes 12296 | tf_op jit(solution)/shard_map/ppermute | solution.py:37
  27.2 1.4 %collective-permute-start.6 = (f32[1,8,1,128]{3,1,2,0:T(8,128)S(1)}, f32[1,8,1,128]{3,1,2,0:T(8,128)S(1)}, u32[]{:S(2)}, u32[]{:S(2)}) collective-permute-start(f32[1,8,1,128]{3,1,2,0:T(8,128)S(1)} %get-tuple-element.63), channel_id=1, source_target_pairs={{1,0},{2,1},{3,2},{0,3},{5,4},{6,5},{7,6},{4,7},{9,8},{10,9},{11,1... | collective-permute-start | bytes 12296 | tf_op jit(solution)/shard_map/ppermute | solution.py:38
  27.3 3.1 %collective-permute-start.7 = (f32[1,8,1,128]{3,1,2,0:T(8,128)S(1)}, f32[1,8,1,128]{3,1,2,0:T(8,128)S(1)}, u32[]{:S(2)}, u32[]{:S(2)}) collective-permute-start(f32[1,8,1,128]{3,1,2,0:T(8,128)S(1)} %get-tuple-element.64), channel_id=1, source_target_pairs={{0,1},{1,2},{2,3},{3,0},{4,5},{5,6},{6,7},{7,4},{8,9},{9,10},{10,1... | collective-permute-start | bytes 12296 | tf_op jit(solution)/shard_map/ppermute | solution.py:37
  32.0 2.1 %copy-start.9 = (f32[8]{0:T(128)S(1)}, f32[8]{0:T(128)}, u32[]{:S(2)}) copy-start(f32[8]{0:T(128)} %constant.109.clone) | copy-start | bytes 100
  32.0 3.7 %collective-permute-start.8 = (f32[1,1,8,128]{3,1,2,0:T(1,128)S(1)}, f32[1,1,8,128]{3,1,2,0:T(1,128)S(1)}, u32[]{:S(2)}, u32[]{:S(2)}) collective-permute-start(f32[1,1,8,128]{3,1,2,0:T(1,128)S(1)} %get-tuple-element.57), channel_id=1, source_target_pairs={{4,0},{8,4},{12,8},{16,12},{20,16},{24,20},{28,24},{0,28},{5,1},{9... | collective-permute-start | bytes 12296 | tf_op jit(solution)/shard_map/ppermute | solution.py:38
  32.1 6.4 %collective-permute-start.9 = (f32[1,1,8,128]{3,1,2,0:T(1,128)S(1)}, f32[1,1,8,128]{3,1,2,0:T(1,128)S(1)}, u32[]{:S(2)}, u32[]{:S(2)}) collective-permute-start(f32[1,1,8,128]{3,1,2,0:T(1,128)S(1)} %get-tuple-element.58), channel_id=1, source_target_pairs={{0,4},{4,8},{8,12},{12,16},{16,20},{20,24},{24,28},{28,0},{1,5},{5... | collective-permute-start | bytes 12296 | tf_op jit(solution)/shard_map/ppermute | solution.py:37
  34.1 4.9 %copy-start.5 = (f32[8,8,128]{2,1,0:T(8,128)S(1)}, f32[8,8,128]{2,1,0:T(8,128)}, u32[]{:S(2)}) copy-start(f32[8,8,128]{2,1,0:T(8,128)} %param.41) | copy-start | bytes 98308
  38.5 0.7 copy-start.7
  38.5 1.4 %collective-permute-start.10 = (f32[1,8,1,128]{3,1,2,0:T(8,128)S(1)}, f32[1,8,1,128]{3,1,2,0:T(8,128)S(1)}, u32[]{:S(2)}, u32[]{:S(2)}) collective-permute-start(f32[1,8,1,128]{3,1,2,0:T(8,128)S(1)} %get-tuple-element.55), channel_id=1, source_target_pairs={{1,0},{2,1},{3,2},{0,3},{5,4},{6,5},{7,6},{4,7},{9,8},{10,9},{11,1... | collective-permute-start | bytes 12296 | tf_op jit(solution)/shard_map/ppermute | solution.py:38
  38.6 3.1 %collective-permute-start.11 = (f32[1,8,1,128]{3,1,2,0:T(8,128)S(1)}, f32[1,8,1,128]{3,1,2,0:T(8,128)S(1)}, u32[]{:S(2)}, u32[]{:S(2)}) collective-permute-start(f32[1,8,1,128]{3,1,2,0:T(8,128)S(1)} %get-tuple-element.56), channel_id=1, source_target_pairs={{0,1},{1,2},{2,3},{3,0},{4,5},{5,6},{6,7},{7,4},{8,9},{9,10},{10,1... | collective-permute-start | bytes 12296 | tf_op jit(solution)/shard_map/ppermute | solution.py:37
  41.9 0.7 copy-start.8
  42.8 0.8 copy-start.11
  43.9 3.7 %collective-permute-start.12 = (f32[2,1,8,128]{3,1,2,0:T(1,128)S(1)}, f32[2,1,8,128]{3,1,2,0:T(1,128)S(1)}, u32[]{:S(2)}, u32[]{:S(2)}) collective-permute-start(f32[2,1,8,128]{3,1,2,0:T(1,128)S(1)} %get-tuple-element.33), channel_id=1, source_target_pairs={{4,0},{8,4},{12,8},{16,12},{20,16},{24,20},{28,24},{0,28},{5,1},{9... | collective-permute-start | bytes 24584 | tf_op jit(solution)/shard_map/ppermute | solution.py:38
  44.0 6.4 %collective-permute-start.13 = (f32[2,1,8,128]{3,1,2,0:T(1,128)S(1)}, f32[2,1,8,128]{3,1,2,0:T(1,128)S(1)}, u32[]{:S(2)}, u32[]{:S(2)}) collective-permute-start(f32[2,1,8,128]{3,1,2,0:T(1,128)S(1)} %get-tuple-element.34), channel_id=1, source_target_pairs={{0,4},{4,8},{8,12},{12,16},{16,20},{20,24},{24,28},{28,0},{1,5},{5... | collective-permute-start | bytes 24584 | tf_op jit(solution)/shard_map/ppermute | solution.py:37
  50.5 1.4 %collective-permute-start.14 = (f32[2,8,1,128]{3,1,2,0:T(8,128)S(1)}, f32[2,8,1,128]{3,1,2,0:T(8,128)S(1)}, u32[]{:S(2)}, u32[]{:S(2)}) collective-permute-start(f32[2,8,1,128]{3,1,2,0:T(8,128)S(1)} %get-tuple-element.31), channel_id=1, source_target_pairs={{1,0},{2,1},{3,2},{0,3},{5,4},{6,5},{7,6},{4,7},{9,8},{10,9},{11,1... | collective-permute-start | bytes 24584 | tf_op jit(solution)/shard_map/ppermute | solution.py:38
  50.5 3.2 %collective-permute-start.15 = (f32[2,8,1,128]{3,1,2,0:T(8,128)S(1)}, f32[2,8,1,128]{3,1,2,0:T(8,128)S(1)}, u32[]{:S(2)}, u32[]{:S(2)}) collective-permute-start(f32[2,8,1,128]{3,1,2,0:T(8,128)S(1)} %get-tuple-element.32), channel_id=1, source_target_pairs={{0,1},{1,2},{2,3},{3,0},{4,5},{5,6},{6,7},{7,4},{8,9},{9,10},{10,1... | collective-permute-start | bytes 24584 | tf_op jit(solution)/shard_map/ppermute | solution.py:37
  54.7 0.7 copy-start.4
  55.6 0.9 copy-start.3
  56.7 3.7 %collective-permute-start.16 = (f32[1,1,8,128]{3,1,2,0:T(1,128)S(1)}, f32[1,1,8,128]{3,1,2,0:T(1,128)S(1)}, u32[]{:S(2)}, u32[]{:S(2)}) collective-permute-start(f32[1,1,8,128]{3,1,2,0:T(1,128)S(1)} %get-tuple-element.49), channel_id=1, source_target_pairs={{4,0},{8,4},{12,8},{16,12},{20,16},{24,20},{28,24},{0,28},{5,1},{9... | collective-permute-start | bytes 12296 | tf_op jit(solution)/shard_map/ppermute | solution.py:38
  56.8 6.4 %collective-permute-start.17 = (f32[1,1,8,128]{3,1,2,0:T(1,128)S(1)}, f32[1,1,8,128]{3,1,2,0:T(1,128)S(1)}, u32[]{:S(2)}, u32[]{:S(2)}) collective-permute-start(f32[1,1,8,128]{3,1,2,0:T(1,128)S(1)} %get-tuple-element.50), channel_id=1, source_target_pairs={{0,4},{4,8},{8,12},{12,16},{16,20},{20,24},{24,28},{28,0},{1,5},{5... | collective-permute-start | bytes 12296 | tf_op jit(solution)/shard_map/ppermute | solution.py:37
  63.2 1.4 %collective-permute-start.18 = (f32[1,8,1,128]{3,1,2,0:T(8,128)S(1)}, f32[1,8,1,128]{3,1,2,0:T(8,128)S(1)}, u32[]{:S(2)}, u32[]{:S(2)}) collective-permute-start(f32[1,8,1,128]{3,1,2,0:T(8,128)S(1)} %get-tuple-element.47), channel_id=1, source_target_pairs={{1,0},{2,1},{3,2},{0,3},{5,4},{6,5},{7,6},{4,7},{9,8},{10,9},{11,1... | collective-permute-start | bytes 12296 | tf_op jit(solution)/shard_map/ppermute | solution.py:38
  63.3 3.1 %collective-permute-start.19 = (f32[1,8,1,128]{3,1,2,0:T(8,128)S(1)}, f32[1,8,1,128]{3,1,2,0:T(8,128)S(1)}, u32[]{:S(2)}, u32[]{:S(2)}) collective-permute-start(f32[1,8,1,128]{3,1,2,0:T(8,128)S(1)} %get-tuple-element.48), channel_id=1, source_target_pairs={{0,1},{1,2},{2,3},{3,0},{4,5},{5,6},{6,7},{7,4},{8,9},{9,10},{10,1... | collective-permute-start | bytes 12296 | tf_op jit(solution)/shard_map/ppermute | solution.py:37
  94.0 3.7 %collective-permute-start.20 = (f32[1,1,8,128]{3,1,2,0:T(1,128)S(1)}, f32[1,1,8,128]{3,1,2,0:T(1,128)S(1)}, u32[]{:S(2)}, u32[]{:S(2)}) collective-permute-start(f32[1,1,8,128]{3,1,2,0:T(1,128)S(1)} %get-tuple-element.41), channel_id=1, source_target_pairs={{4,0},{8,4},{12,8},{16,12},{20,16},{24,20},{28,24},{0,28},{5,1},{9... | collective-permute-start | bytes 12296 | tf_op jit(solution)/shard_map/ppermute | solution.py:38
  96.1 6.3 %collective-permute-start.21 = (f32[1,1,8,128]{3,1,2,0:T(1,128)S(1)}, f32[1,1,8,128]{3,1,2,0:T(1,128)S(1)}, u32[]{:S(2)}, u32[]{:S(2)}) collective-permute-start(f32[1,1,8,128]{3,1,2,0:T(1,128)S(1)} %get-tuple-element.42), channel_id=1, source_target_pairs={{0,4},{4,8},{8,12},{12,16},{16,20},{20,24},{24,28},{28,0},{1,5},{5... | collective-permute-start | bytes 12296 | tf_op jit(solution)/shard_map/ppermute | solution.py:37
  102.4 1.4 %collective-permute-start.22 = (f32[1,8,1,128]{3,1,2,0:T(8,128)S(1)}, f32[1,8,1,128]{3,1,2,0:T(8,128)S(1)}, u32[]{:S(2)}, u32[]{:S(2)}) collective-permute-start(f32[1,8,1,128]{3,1,2,0:T(8,128)S(1)} %get-tuple-element.39), channel_id=1, source_target_pairs={{1,0},{2,1},{3,2},{0,3},{5,4},{6,5},{7,6},{4,7},{9,8},{10,9},{11,1... | collective-permute-start | bytes 12296 | tf_op jit(solution)/shard_map/ppermute | solution.py:38
  102.5 3.1 %collective-permute-start.23 = (f32[1,8,1,128]{3,1,2,0:T(8,128)S(1)}, f32[1,8,1,128]{3,1,2,0:T(8,128)S(1)}, u32[]{:S(2)}, u32[]{:S(2)}) collective-permute-start(f32[1,8,1,128]{3,1,2,0:T(8,128)S(1)} %get-tuple-element.40), channel_id=1, source_target_pairs={{0,1},{1,2},{2,3},{3,0},{4,5},{5,6},{6,7},{7,4},{8,9},{9,10},{10,1... | collective-permute-start | bytes 12296 | tf_op jit(solution)/shard_map/ppermute | solution.py:37
